TPU v7x, 128 devices: a whole 4x4x4 slice. The times are simulated.
128 devices in a mesh: lon: 32 (over z, y_lo, x), ch: 4 (over y_hi, core).
Axes of the slice: x: 4, y: 4 (y_hi: 2, y_lo: 2; y = y_hi * 2 + y_lo), z: 4, core: 2. Of those that a mesh axis runs over, the one named last changes fastest.
Arguments:
- grid_inputs: bfloat16 [921600, 474], P('lon'), may hold values from -6 to 6
- embed_weight: bfloat16 [474, 512], replicated, may hold values from -0.25 to 0.25
- embed_bias: float32 [512], replicated, may hold values from -3 to 3
- mesh_latent: bfloat16 [20480, 512], P('lon', 'ch'), may hold values from -6 to 6
- edge_features: bfloat16 [4, 720896], P(None, 'lon'), may hold values from -6 to 6
- senders: int32 [720896], P('lon'), may hold values from 0 to 921599, as said below
- receivers: int32 [720896], P('lon'), may hold values from 0 to 20479, as said below
- sender_weight: bfloat16 [512, 512], P(None, 'ch'), may hold values from -0.25 to 0.25
- receiver_weight: bfloat16 [512, 512], P(None, 'ch'), may hold values from -0.25 to 0.25
- feature_weight: bfloat16 [4, 512], P(None, 'ch'), may hold values from -3 to 3
- hidden_bias: float32 [512], P('ch'), may hold values from -3 to 3
- message_weight: bfloat16 [512, 512], P('ch'), may hold values from -0.25 to 0.25
- message_bias: float32 [512], replicated, may hold values from -1.2 to 1.2
- norm_gain: float32 [512], P('ch'), may hold values from 0.5 to 1.5
- norm_shift: float32 [512], P('ch'), may hold values from -3 to 3
Outputs:
- mesh_out: bfloat16 [20480, 512], P('lon', 'ch')
Inputs may be any that keep to these rules, and one draw needn't show every extreme that they name: Edge e belongs to block b = e // 22528. Its sender is c * 640 + t with latitude row t and a column c that lies, counted around the closed circle of 1440 columns, at most 4 columns before or after the block's own columns b * 45 to b * 45 + 44; some block reaches 4 columns on both sides. Within each aligned run of min(2048, 22528) edges of a block, the senders' columns, counted from the block's first widened column, lie within 7 consecutive columns. `receivers`: the receiver of edge e lies among the mesh nodes b * 640 to b * 640 + 639 of its block b = e // 22528; a mesh node may receive no edge.
All inputs are finite; a program needn't handle non-finite values.
Results may differ from a plain program's by a relative error of at most 0.0028.
Values may be sent and summed in bfloat16 or wider, within the bound.
No kernel may reach another device: no remote copies, remote signals or barrier semaphores. Data moves between devices by JAX's collectives and lax.ppermute only.
A program may use at most 128 MiB of HBM per device.

v0:
```python
import jax
import jax.numpy as jnp
from jax import lax
from jax.sharding import PartitionSpec as P

LAT = 640
HALO = 4


def with_halo(block, sides, width):
    for axis, dim in sides:
        count = lax.axis_size(axis)
        forward = [(i, i + 1) for i in range(count - 1)]
        forward.append((count - 1, 0))
        backward = [(target, source) for source, target in forward]
        low = lax.ppermute(
            lax.slice_in_dim(block, block.shape[dim] - width, None, axis=dim), axis, forward
        )
        high = lax.ppermute(lax.slice_in_dim(block, 0, width, axis=dim), axis, backward)
        block = jnp.concatenate([low, block, high], axis=dim)
    return block


def split_up(value, dim, devices):
    before, after = (value.shape[:dim], value.shape[dim + 1 :])
    return jnp.moveaxis(value.reshape(*before, devices, -1, *after), dim, 0)


def sent_and_summed(value, axis, dim):
    devices = lax.axis_size(axis)
    parts = lax.all_to_all(split_up(value, dim, devices), axis, 0, 0, tiled=True)
    return jnp.sum(parts, axis=0)


def embedded(grid_rows, embed_weight, embed_bias):
    return jax.nn.silu(
        jnp.dot(grid_rows, embed_weight, preferred_element_type=jnp.float32) + embed_bias
    ).astype(jnp.bfloat16)


def on_device(
    grid_inputs,
    embed_weight,
    embed_bias,
    mesh_latent,
    edge_features,
    senders,
    receivers,
    sender_weight,
    receiver_weight,
    feature_weight,
    hidden_bias,
    message_weight,
    message_bias,
    norm_gain,
    norm_shift,
):
    lon_count = lax.axis_size("lon")
    lon_place = lax.axis_index("lon")
    ch_place = lax.axis_index("ch")
    columns = grid_inputs.shape[0] // LAT
    mesh_nodes = mesh_latent.shape[0]
    share_width = mesh_latent.shape[1]
    full_width = message_weight.shape[1]
    latent = embedded(grid_inputs, embed_weight, embed_bias)
    own_terms = jnp.dot(latent, sender_weight, preferred_element_type=jnp.float32)
    widened = with_halo(
        own_terms.reshape(columns, LAT, share_width).astype(jnp.bfloat16), (("lon", 0),), HALO
    ).astype(jnp.float32)
    sent_terms = widened.reshape(-1, share_width)
    grid_column = senders // LAT
    shifted = jnp.mod(grid_column - lon_place * columns + HALO, columns * lon_count)
    local_send = shifted * LAT + senders % LAT
    local_recv = receivers - lon_place * mesh_nodes
    full_mesh = lax.all_gather(mesh_latent, "ch", axis=1, tiled=True)
    recv_terms = jnp.dot(full_mesh, receiver_weight, preferred_element_type=jnp.float32)
    edge_count = senders.shape[0]
    block_rows = min(2048, edge_count)
    steps_count = edge_count // block_rows
    feature_blocks = jnp.transpose(
        edge_features.reshape(edge_features.shape[0], steps_count, block_rows), (1, 0, 2)
    )
    node_ids = lax.broadcasted_iota(jnp.int32, (1, mesh_nodes), 1)

    def accumulate(carried, pieces):
        totals, tallies = carried
        send_ids, recv_ids, features = pieces
        before = jnp.take(sent_terms, send_ids, axis=0) + jnp.take(recv_terms, recv_ids, axis=0)
        before = (
            before
            + lax.dot_general(
                features,
                feature_weight,
                (((0,), (0,)), ((), ())),
                preferred_element_type=jnp.float32,
            )
            + hidden_bias
        )
        hidden = jax.nn.silu(before).astype(jnp.bfloat16)
        one_hot = (recv_ids[:, None] == node_ids).astype(jnp.bfloat16)
        totals = totals + lax.dot_general(
            one_hot, hidden, (((0,), (0,)), ((), ())), preferred_element_type=jnp.float32
        )
        tallies = tallies + jnp.sum(one_hot, axis=0, dtype=jnp.float32)
        return ((totals, tallies), None)

    start = (
        jnp.zeros((mesh_nodes, share_width), jnp.float32),
        jnp.zeros((mesh_nodes,), jnp.float32),
    )
    pieces_all = (
        local_send.reshape(steps_count, block_rows),
        local_recv.reshape(steps_count, block_rows),
        feature_blocks,
    )
    (totals, tallies), ignored = lax.scan(accumulate, start, pieces_all)
    partial_value = jnp.dot(
        totals, message_weight.astype(jnp.float32), precision=lax.Precision.HIGHEST
    )
    bias_share = lax.dynamic_slice_in_dim(message_bias, ch_place * share_width, share_width, 0)
    node_share = sent_and_summed(partial_value, "ch", 1) + tallies[:, None] * bias_share
    first_sum, second = lax.psum(
        (
            jnp.sum(node_share, axis=1, keepdims=True),
            jnp.sum(jnp.square(node_share), axis=1, keepdims=True),
        ),
        "ch",
    )
    centre = first_sum / full_width
    spread = second / full_width - jnp.square(centre)
    normed = (node_share - centre) * lax.rsqrt(spread + 1.0)
    return (mesh_latent.astype(jnp.float32) + normed * norm_gain + norm_shift).astype(jnp.bfloat16)


def solution(mesh):
    return jax.shard_map(
        on_device,
        mesh=mesh,
        in_specs=(
            P("lon", None),
            P(),
            P(),
            P("lon", "ch"),
            P(None, "lon"),
            P("lon"),
            P("lon"),
            P(None, "ch"),
            P(None, "ch"),
            P(None, "ch"),
            P("ch"),
            P("ch", None),
            P(),
            P("ch"),
            P("ch"),
        ),
        out_specs=P("lon", "ch"),
        check_vma=False,
    )
```

profile of v0, /device:TPU:1, one launch (start us, length us, event | category | flops | bytes accessed | tf_op | source)
XLA Modules:
  0.0 352.2 jit_solution(3035467392577934759)
XLA Ops:
  1.0 31.8 %multiply_convert_fusion.1 = bf16[28800,512]{1,0:T(8,128)(2,1)} fusion(bf16[28800,474]{0,1:T(8,128)(2,1)} %param.17, bf16[474,512]{1,0:T(8,128)(2,1)S(1)} %copy-done, f32[512]{0:T(512)} %param.19), kind=kOutput, calls=%fused_computation.33 | convolution fusion | flops 14067302400 | bytes 57281024 | tf_op jit(solution)/shard_map/dot_general | solution.py:37
  32.8 13.5 %convolution_convert_fusion = bf16[28800,128]{1,0:T(8,128)(2,1)S(1)} fusion(bf16[28800,512]{1,0:T(8,128)(2,1)} %multiply_convert_fusion.1, bf16[512,128]{1,0:T(8,128)(2,1)S(1)} %copy-done.4), kind=kOutput, calls=%fused_computation.34 | convolution fusion | flops 3778560000 | bytes 36995072 | tf_op jit(solution)/shard_map/dot_general | solution.py:66
  52.5 5.8 %collective-permute-start.1 = (bf16[4,640,128]{2,1,0:T(8,128)(2,1)}, bf16[4,640,128]{2,1,0:T(8,128)(2,1)S(1)}, u32[]{:S(2)}, u32[]{:S(2)}) collective-permute-start(bf16[4,640,128]{2,1,0:T(8,128)(2,1)} %bitcast.2), channel_id=1, source_target_pairs={{4,0},{8,4},{12,8},{16,12},{20,16},{24,20},{28,24},{32,28},{36,32}... | collective-permute-start | bytes 1966088 | tf_op jit(solution)/shard_map/ppermute | solution.py:19
  58.5 18.9 %all_gather.3 = bf16[640,512]{1,0:T(8,128)(2,1)S(1)} all-gather(bf16[640,128]{1,0:T(8,128)(2,1)S(1)} %copy-done.3), channel_id=1, replica_groups=mesh['lon'=32,'ch'=4] {'ch'}, dimensions={1}, use_global_device_ids=true | all-gather | bytes 819200 | tf_op jit(solution)/shard_map/all_gather | solution.py:75
  77.8 4.3 %pad_maximum_fusion = bf16[53,640,128]{2,1,0:T(8,128)(2,1)S(1)} fusion(bf16[4,640,128]{2,1,0:T(8,128)(2,1)S(1)} %collective-permute-done.1, bf16[45,640,128]{2,1,0:T(8,128)(2,1)} %bitcast.47, bf16[4,640,128]{2,1,0:T(8,128)(2,1)S(1)} %collective-permute-done), kind=kLoop, calls=%fused_computation.35 | loop fusion | flops 8683520 | bytes 17367040 | tf_op jit(solution)/shard_map/concatenate | solution.py:20
  82.1 6.2 %bitcast_convert_fusion = f32[33920,128]{1,0:T(8,128)} fusion(bf16[53,640,128]{2,1,0:T(8,128)(2,1)S(1)} %pad_maximum_fusion), kind=kLoop, calls=%fused_computation.36 | loop fusion | flops 4341760 | bytes 26050560 | tf_op jit(solution)/shard_map/convert_element_type | solution.py:69
  88.3 231.8 %while.13 = (s32[]{:T(128)}, f32[640,128]{1,0:T(8,128)S(1)}, f32[640]{0:T(1024)S(1)}, s32[11,2048]{1,0:T(8,128)S(1)}, s32[11,2048]{1,0:T(8,128)S(1)}, /*index=5*...) while((s32[]{:T(128)}, f32[640,128]{1,0:T(8,128)S(1)}, ...), condition=%wide.region_2.3_spmd.clone, body=%wide.region_0.2_spmd.clone.sunk | while | flops 347021952 | bytes 7114884 | solution.py:116
  88.4 5.5 %gather_fusion = f32[2048,128]{1,0:T(8,128)S(1)} fusion(f32[640,128]{1,0:T(8,128)S(1)} %get-tuple-element.233, s32[2048]{0:T(1024)S(1)} %broadcast_clamp_fusion.4), kind=kCustom, calls=%fused_computation.1.clone.clone.1 | custom fusion | bytes 2105344 | tf_op jit(solution)/shard_map/while/body/eval_jaxpr/jit(_take)/gather | solution.py:88
  93.9 11.4 %gather_fusion.1 = f32[2048,128]{1,0:T(8,128)S(1)} fusion(f32[33920,128]{1,0:T(8,128)} %get-tuple-element.232, s32[2048]{0:T(1024)S(1)} %broadcast_clamp_fusion.5), kind=kCustom, calls=%fused_computation.clone.clone.1 | custom fusion | bytes 2105344 | tf_op jit(solution)/shard_map/while/body/eval_jaxpr/jit(_take)/gather | solution.py:88
  109.4 5.5 %gather_fusion = f32[2048,128]{1,0:T(8,128)S(1)} fusion(f32[640,128]{1,0:T(8,128)S(1)} %get-tuple-element.233, s32[2048]{0:T(1024)S(1)} %broadcast_clamp_fusion.4), kind=kCustom, calls=%fused_computation.1.clone.clone.1 | custom fusion | bytes 2105344 | tf_op jit(solution)/shard_map/while/body/eval_jaxpr/jit(_take)/gather | solution.py:88
  114.9 11.4 %gather_fusion.1 = f32[2048,128]{1,0:T(8,128)S(1)} fusion(f32[33920,128]{1,0:T(8,128)} %get-tuple-element.232, s32[2048]{0:T(1024)S(1)} %broadcast_clamp_fusion.5), kind=kCustom, calls=%fused_computation.clone.clone.1 | custom fusion | bytes 2105344 | tf_op jit(solution)/shard_map/while/body/eval_jaxpr/jit(_take)/gather | solution.py:88
  130.5 5.5 %gather_fusion = f32[2048,128]{1,0:T(8,128)S(1)} fusion(f32[640,128]{1,0:T(8,128)S(1)} %get-tuple-element.233, s32[2048]{0:T(1024)S(1)} %broadcast_clamp_fusion.4), kind=kCustom, calls=%fused_computation.1.clone.clone.1 | custom fusion | bytes 2105344 | tf_op jit(solution)/shard_map/while/body/eval_jaxpr/jit(_take)/gather | solution.py:88
  136.0 11.4 %gather_fusion.1 = f32[2048,128]{1,0:T(8,128)S(1)} fusion(f32[33920,128]{1,0:T(8,128)} %get-tuple-element.232, s32[2048]{0:T(1024)S(1)} %broadcast_clamp_fusion.5), kind=kCustom, calls=%fused_computation.clone.clone.1 | custom fusion | bytes 2105344 | tf_op jit(solution)/shard_map/while/body/eval_jaxpr/jit(_take)/gather | solution.py:88
  151.6 5.5 %gather_fusion = f32[2048,128]{1,0:T(8,128)S(1)} fusion(f32[640,128]{1,0:T(8,128)S(1)} %get-tuple-element.233, s32[2048]{0:T(1024)S(1)} %broadcast_clamp_fusion.4), kind=kCustom, calls=%fused_computation.1.clone.clone.1 | custom fusion | bytes 2105344 | tf_op jit(solution)/shard_map/while/body/eval_jaxpr/jit(_take)/gather | solution.py:88
  157.1 11.4 %gather_fusion.1 = f32[2048,128]{1,0:T(8,128)S(1)} fusion(f32[33920,128]{1,0:T(8,128)} %get-tuple-element.232, s32[2048]{0:T(1024)S(1)} %broadcast_clamp_fusion.5), kind=kCustom, calls=%fused_computation.clone.clone.1 | custom fusion | bytes 2105344 | tf_op jit(solution)/shard_map/while/body/eval_jaxpr/jit(_take)/gather | solution.py:88
  172.6 5.5 %gather_fusion = f32[2048,128]{1,0:T(8,128)S(1)} fusion(f32[640,128]{1,0:T(8,128)S(1)} %get-tuple-element.233, s32[2048]{0:T(1024)S(1)} %broadcast_clamp_fusion.4), kind=kCustom, calls=%fused_computation.1.clone.clone.1 | custom fusion | bytes 2105344 | tf_op jit(solution)/shard_map/while/body/eval_jaxpr/jit(_take)/gather | solution.py:88
  178.1 11.4 %gather_fusion.1 = f32[2048,128]{1,0:T(8,128)S(1)} fusion(f32[33920,128]{1,0:T(8,128)} %get-tuple-element.232, s32[2048]{0:T(1024)S(1)} %broadcast_clamp_fusion.5), kind=kCustom, calls=%fused_computation.clone.clone.1 | custom fusion | bytes 2105344 | tf_op jit(solution)/shard_map/while/body/eval_jaxpr/jit(_take)/gather | solution.py:88
  193.7 5.5 %gather_fusion = f32[2048,128]{1,0:T(8,128)S(1)} fusion(f32[640,128]{1,0:T(8,128)S(1)} %get-tuple-element.233, s32[2048]{0:T(1024)S(1)} %broadcast_clamp_fusion.4), kind=kCustom, calls=%fused_computation.1.clone.clone.1 | custom fusion | bytes 2105344 | tf_op jit(solution)/shard_map/while/body/eval_jaxpr/jit(_take)/gather | solution.py:88
  199.2 11.4 %gather_fusion.1 = f32[2048,128]{1,0:T(8,128)S(1)} fusion(f32[33920,128]{1,0:T(8,128)} %get-tuple-element.232, s32[2048]{0:T(1024)S(1)} %broadcast_clamp_fusion.5), kind=kCustom, calls=%fused_computation.clone.clone.1 | custom fusion | bytes 2105344 | tf_op jit(solution)/shard_map/while/body/eval_jaxpr/jit(_take)/gather | solution.py:88
  214.8 5.5 %gather_fusion = f32[2048,128]{1,0:T(8,128)S(1)} fusion(f32[640,128]{1,0:T(8,128)S(1)} %get-tuple-element.233, s32[2048]{0:T(1024)S(1)} %broadcast_clamp_fusion.4), kind=kCustom, calls=%fused_computation.1.clone.clone.1 | custom fusion | bytes 2105344 | tf_op jit(solution)/shard_map/while/body/eval_jaxpr/jit(_take)/gather | solution.py:88
  220.3 11.4 %gather_fusion.1 = f32[2048,128]{1,0:T(8,128)S(1)} fusion(f32[33920,128]{1,0:T(8,128)} %get-tuple-element.232, s32[2048]{0:T(1024)S(1)} %broadcast_clamp_fusion.5), kind=kCustom, calls=%fused_computation.clone.clone.1 | custom fusion | bytes 2105344 | tf_op jit(solution)/shard_map/while/body/eval_jaxpr/jit(_take)/gather | solution.py:88
  235.9 5.5 %gather_fusion = f32[2048,128]{1,0:T(8,128)S(1)} fusion(f32[640,128]{1,0:T(8,128)S(1)} %get-tuple-element.233, s32[2048]{0:T(1024)S(1)} %broadcast_clamp_fusion.4), kind=kCustom, calls=%fused_computation.1.clone.clone.1 | custom fusion | bytes 2105344 | tf_op jit(solution)/shard_map/while/body/eval_jaxpr/jit(_take)/gather | solution.py:88
  241.4 11.4 %gather_fusion.1 = f32[2048,128]{1,0:T(8,128)S(1)} fusion(f32[33920,128]{1,0:T(8,128)} %get-tuple-element.232, s32[2048]{0:T(1024)S(1)} %broadcast_clamp_fusion.5), kind=kCustom, calls=%fused_computation.clone.clone.1 | custom fusion | bytes 2105344 | tf_op jit(solution)/shard_map/while/body/eval_jaxpr/jit(_take)/gather | solution.py:88
  256.9 5.5 %gather_fusion = f32[2048,128]{1,0:T(8,128)S(1)} fusion(f32[640,128]{1,0:T(8,128)S(1)} %get-tuple-element.233, s32[2048]{0:T(1024)S(1)} %broadcast_clamp_fusion.4), kind=kCustom, calls=%fused_computation.1.clone.clone.1 | custom fusion | bytes 2105344 | tf_op jit(solution)/shard_map/while/body/eval_jaxpr/jit(_take)/gather | solution.py:88
  262.4 11.4 %gather_fusion.1 = f32[2048,128]{1,0:T(8,128)S(1)} fusion(f32[33920,128]{1,0:T(8,128)} %get-tuple-element.232, s32[2048]{0:T(1024)S(1)} %broadcast_clamp_fusion.5), kind=kCustom, calls=%fused_computation.clone.clone.1 | custom fusion | bytes 2105344 | tf_op jit(solution)/shard_map/while/body/eval_jaxpr/jit(_take)/gather | solution.py:88
  278.0 5.5 %gather_fusion = f32[2048,128]{1,0:T(8,128)S(1)} fusion(f32[640,128]{1,0:T(8,128)S(1)} %get-tuple-element.233, s32[2048]{0:T(1024)S(1)} %broadcast_clamp_fusion.4), kind=kCustom, calls=%fused_computation.1.clone.clone.1 | custom fusion | bytes 2105344 | tf_op jit(solution)/shard_map/while/body/eval_jaxpr/jit(_take)/gather | solution.py:88
  283.5 11.4 %gather_fusion.1 = f32[2048,128]{1,0:T(8,128)S(1)} fusion(f32[33920,128]{1,0:T(8,128)} %get-tuple-element.232, s32[2048]{0:T(1024)S(1)} %broadcast_clamp_fusion.5), kind=kCustom, calls=%fused_computation.clone.clone.1 | custom fusion | bytes 2105344 | tf_op jit(solution)/shard_map/while/body/eval_jaxpr/jit(_take)/gather | solution.py:88
  299.1 5.5 %gather_fusion = f32[2048,128]{1,0:T(8,128)S(1)} fusion(f32[640,128]{1,0:T(8,128)S(1)} %get-tuple-element.233, s32[2048]{0:T(1024)S(1)} %broadcast_clamp_fusion.4), kind=kCustom, calls=%fused_computation.1.clone.clone.1 | custom fusion | bytes 2105344 | tf_op jit(solution)/shard_map/while/body/eval_jaxpr/jit(_take)/gather | solution.py:88
  304.6 11.4 %gather_fusion.1 = f32[2048,128]{1,0:T(8,128)S(1)} fusion(f32[33920,128]{1,0:T(8,128)} %get-tuple-element.232, s32[2048]{0:T(1024)S(1)} %broadcast_clamp_fusion.5), kind=kCustom, calls=%fused_computation.clone.clone.1 | custom fusion | bytes 2105344 | tf_op jit(solution)/shard_map/while/body/eval_jaxpr/jit(_take)/gather | solution.py:88
  321.9 3.7 %all-to-all-start = ((f32[4,640,128]{1,2,0:T(8,128)}), f32[4,640,128]{1,2,0:T(8,128)S(1)}, u32[]{:S(2)}, u32[]{:S(2)}) async-start(f32[4,640,128]{1,2,0:T(8,128)} %bitcast.7), calls=%async_computation | async-start | bytes 2621440 | tf_op jit(solution)/shard_map/all_to_all | solution.py:31
  326.5 16.9 %all-to-all-done = f32[4,640,128]{1,2,0:T(8,128)S(1)} async-done(((f32[4,640,128]{1,2,0:T(8,128)}), f32[4,640,128]{1,2,0:T(8,128)S(1)}, u32[]{:S(2)}, u32[]{:S(2)}) %all-to-all-start) | async-done | bytes 1310752 | tf_op jit(solution)/shard_map/all_to_all | solution.py:31
  343.6 7.5 %all-reduce = (f32[640,1]{0,1:T(1,128)S(1)}, f32[640,1]{0,1:T(1,128)S(1)}) all-reduce(f32[640,1]{0,1:T(1,128)S(1)} %broadcast_in_dim.39, f32[640,1]{0,1:T(1,128)S(1)} %broadcast_in_dim.40), channel_id=1, replica_groups=mesh['lon'=32,'ch'=4] {'ch'}, use_global_device_ids=true, to_apply=%region_5.6 | all-reduce | flops 1280 | bytes 10240 | tf_op jit(solution)/shard_map/psum | solution.py:122
  (135 shorter events, 57.0 us)
Async XLA Ops:
  0.0 1.0 copy-start
  0.0 32.8 %copy-start.4 = (bf16[512,128]{1,0:T(8,128)(2,1)S(1)}, bf16[512,128]{1,0:T(8,128)(2,1)}, u32[]{:S(2)}) copy-start(bf16[512,128]{1,0:T(8,128)(2,1)} %param.24) | copy-start | bytes 393220
  32.8 25.4 %copy-start.7 = (s32[22528]{0:T(1024)S(1)}, s32[22528]{0:T(1024)}, u32[]{:S(2)}) copy-start(s32[22528]{0:T(1024)} %param.23) | copy-start | bytes 270340
  32.8 25.5 %copy-start.8 = (s32[22528]{0:T(1024)S(1)}, s32[22528]{0:T(1024)}, u32[]{:S(2)}) copy-start(s32[22528]{0:T(1024)} %param.22) | copy-start | bytes 270340
  32.8 25.7 %copy-start.3 = (bf16[640,128]{1,0:T(8,128)(2,1)S(1)}, bf16[640,128]{1,0:T(8,128)(2,1)}, u32[]{:S(2)}) copy-start(bf16[640,128]{1,0:T(8,128)(2,1)} %param.20) | copy-start | bytes 491524
  32.8 44.6 %copy-start.5 = (bf16[512,128]{1,0:T(8,128)(2,1)S(1)}, bf16[512,128]{1,0:T(8,128)(2,1)}, u32[]{:S(2)}) copy-start(bf16[512,128]{1,0:T(8,128)(2,1)} %param.25) | copy-start | bytes 393220
  46.3 3.0 copy-start.2
  50.4 27.3 %collective-permute-start = (bf16[4,640,128]{2,1,0:T(8,128)(2,1)}, bf16[4,640,128]{2,1,0:T(8,128)(2,1)S(1)}, u32[]{:S(2)}, u32[]{:S(2)}) collective-permute-start(bf16[4,640,128]{2,1,0:T(8,128)(2,1)} %bitcast), channel_id=1, source_target_pairs={{0,4},{4,8},{8,12},{12,16},{16,20},{20,24},{24,28},{28,32},{32,36}... | collective-permute-start | bytes 1966088 | tf_op jit(solution)/shard_map/ppermute | solution.py:16
  52.5 25.3 %collective-permute-start.1 = (bf16[4,640,128]{2,1,0:T(8,128)(2,1)}, bf16[4,640,128]{2,1,0:T(8,128)(2,1)S(1)}, u32[]{:S(2)}, u32[]{:S(2)}) collective-permute-start(bf16[4,640,128]{2,1,0:T(8,128)(2,1)} %bitcast.2), channel_id=1, source_target_pairs={{4,0},{8,4},{12,8},{16,12},{20,16},{24,20},{28,24},{32,28},{36,32}... | collective-permute-start | bytes 1966088 | tf_op jit(solution)/shard_map/ppermute | solution.py:19
  82.1 6.2 %copy-start.11 = (bf16[4,128]{1,0:T(4,128)(2,1)S(1)}, bf16[4,128]{1,0:T(4,128)(2,1)}, u32[]{:S(2)}) copy-start(bf16[4,128]{1,0:T(4,128)(2,1)} %param.26) | copy-start | bytes 3076
  82.1 6.2 %copy-start.12 = (f32[128]{0:T(128)S(1)}, f32[128]{0:T(128)}, u32[]{:S(2)}) copy-start(f32[128]{0:T(128)} %param.27) | copy-start | bytes 1540
  88.3 231.8 %copy-start.6 = (bf16[128,512]{1,0:T(8,128)(2,1)S(1)}, bf16[128,512]{1,0:T(8,128)(2,1)}, u32[]{:S(2)}) copy-start(bf16[128,512]{1,0:T(8,128)(2,1)} %param.28) | copy-start | bytes 393220
  88.3 262.9 %copy-start.9 = (f32[128]{0:T(128)S(1)}, f32[128]{0:T(128)}, u32[]{:S(2)}) copy-start(f32[128]{0:T(128)} %param.31) | copy-start | bytes 1540
  88.3 262.9 %copy-start.10 = (f32[128]{0:T(128)S(1)}, f32[128]{0:T(128)}, u32[]{:S(2)}) copy-start(f32[128]{0:T(128)} %param.30) | copy-start | bytes 1540
  320.1 32.1 %copy-start.1 = (bf16[474,512]{1,0:T(8,128)(2,1)S(1)}, bf16[474,512]{1,0:T(8,128)(2,1)}, u32[]{:S(2)}) copy-start(bf16[474,512]{1,0:T(8,128)(2,1)} %param.18) | copy-start | bytes 1456132
  321.9 21.4 %all-to-all-start = ((f32[4,640,128]{1,2,0:T(8,128)}), f32[4,640,128]{1,2,0:T(8,128)S(1)}, u32[]{:S(2)}, u32[]{:S(2)}) async-start(f32[4,640,128]{1,2,0:T(8,128)} %bitcast.7), calls=%async_computation | async-start | bytes 2621440 | tf_op jit(solution)/shard_map/all_to_all | solution.py:31
where the time goes:
time: 353 us; the launch traced here: 352 us
  local copies, waits for them, and re-layouts  193 us (55%)
  matrix products  84.4 us (24%)
  blocking collectives  26.4 us (7%)
  other arithmetic  19.2 us (5%)
  waiting for transfers between devices  16.9 us (5%)
  starting transfers between devices  11.4 us (3%)
    gather x11, local copies, waits for them, and re-layouts, accumulate(): jnp.take(sent_terms, send_ids, axis=0)  125 us
    gather x11, local copies, waits for them, and re-layouts, accumulate(): jnp.take(recv_terms, recv_ids, axis=0)  60.1 us
    dot_general x11, matrix products, accumulate(): lax.dot_general(one_hot, hidden, (((0,), (0,)), ((), ())), preferred_elem...  37.1 us
    dot_general x1, matrix products, embedded(): jnp.dot(grid_rows, embed_weight, preferred_element_type=jnp.float32)  31.8 us
    all_gather x1, blocking collectives, on_device(): full_mesh = lax.all_gather(mesh_latent, 'ch', axis=1, tiled=True)  18.9 us
    all_to_all x1, waiting for transfers between devices, sent_and_summed(): lax.all_to_all(split_up(value, dim, devices), axis, 0, 0, tiled=True)  16.9 us
    dot_general x1, matrix products, on_device(): jnp.dot(latent, sender_weight, preferred_element_type=jnp.float32)  13.5 us
    psum x1, blocking collectives, on_device(): lax.psum((jnp.sum(node_share, axis=1, keepdims=True), jnp.sum(jnp.square(...  7.53 us
  transfers between devices with their start and end apart: 3, of which 1 were waited for; matrix products, arithmetic and copies ran while one was open for 0% of the time, Pallas kernels for 0%

commit v1 on v0

--- a/solution.py
+++ b/solution.py
@@ -72,7 +72,9 @@
     shifted = jnp.mod(grid_column - lon_place * columns + HALO, columns * lon_count)
     local_send = shifted * LAT + senders % LAT
     local_recv = receivers - lon_place * mesh_nodes
-    full_mesh = lax.all_gather(mesh_latent, "ch", axis=1, tiled=True)
+    full_mesh = jnp.concatenate(
+        lax.all_to_all(jnp.stack([mesh_latent] * lax.axis_size("ch")), "ch", 0, 0), axis=1
+    )
     recv_terms = jnp.dot(full_mesh, receiver_weight, preferred_element_type=jnp.float32)
     edge_count = senders.shape[0]
     block_rows = min(2048, edge_count)

time: 353 us -> 359 us (1.017)
  blocking collectives: 26.4 us -> 7.53 us
  waiting for transfers between devices: 16.9 us -> 32 us
  starting transfers between devices: 11.4 us -> 16.9 us
    all_gather x1 -> x0, blocking collectives: 18.9 us -> none  [on_device(): full_mesh = lax.all_gather(mesh_latent, 'ch', axis=1, tiled=True)]
    all_to_all x0 -> x1, waiting for transfers between devices: none -> 15 us  [on_device(): lax.all_to_all(jnp.stack([mesh_latent] * lax.axis_size('ch')), 'ch', 0, 0)]
    all_to_all x0 -> x1, starting transfers between devices: none -> 5.13 us  [on_device(): lax.all_to_all(jnp.stack([mesh_latent] * lax.axis_size('ch')), 'ch', 0, 0)]
  transfers between devices with their start and end apart: 3 -> 4, of which waited for: 1 -> 2; matrix products, arithmetic and copies ran while one was open for 0% -> 1% of each run, Pallas kernels for 0% -> 0%
where the time goes in v1:
time: 359 us; the launch traced here: 355 us
  local copies, waits for them, and re-layouts  194 us (54%)
  matrix products  84.5 us (24%)
  waiting for transfers between devices  32 us (9%)
  other arithmetic  19.2 us (5%)
  starting transfers between devices  16.9 us (5%)
  blocking collectives  7.53 us (2%)
    gather x11, local copies, waits for them, and re-layouts, accumulate(): jnp.take(sent_terms, send_ids, axis=0)  125 us
    gather x11, local copies, waits for them, and re-layouts, accumulate(): jnp.take(recv_terms, recv_ids, axis=0)  60.1 us
    dot_general x11, matrix products, accumulate(): lax.dot_general(one_hot, hidden, (((0,), (0,)), ((), ())), preferred_elem...  37.1 us
    dot_general x1, matrix products, embedded(): jnp.dot(grid_rows, embed_weight, preferred_element_type=jnp.float32)  31.7 us
    all_to_all x1, waiting for transfers between devices, sent_and_summed(): lax.all_to_all(split_up(value, dim, devices), axis, 0, 0, tiled=True)  17 us
    all_to_all x1, waiting for transfers between devices, on_device(): lax.all_to_all(jnp.stack([mesh_latent] * lax.axis_size('ch')), 'ch', 0, 0)  15 us
    dot_general x1, matrix products, on_device(): jnp.dot(latent, sender_weight, preferred_element_type=jnp.float32)  13.5 us
    psum x1, blocking collectives, on_device(): lax.psum((jnp.sum(node_share, axis=1, keepdims=True), jnp.sum(jnp.square(...  7.53 us
  transfers between devices with their start and end apart: 4, of which 2 were waited for; matrix products, arithmetic and copies ran while one was open for 1% of the time, Pallas kernels for 0%

profile of v1, /device:TPU:1, one launch (start us, length us, event | category | flops | bytes accessed | tf_op | source)
XLA Modules:
  0.0 354.9 jit_solution(12217390365969735245)
XLA Ops:
  1.0 31.7 %multiply_convert_fusion.1 = bf16[28800,512]{1,0:T(8,128)(2,1)} fusion(bf16[28800,474]{0,1:T(8,128)(2,1)} %param.17, bf16[474,512]{1,0:T(8,128)(2,1)S(1)} %copy-done, f32[512]{0:T(512)} %param.19), kind=kOutput, calls=%fused_computation.33 | convolution fusion | flops 14067302400 | bytes 57281024 | tf_op jit(solution)/shard_map/dot_general | solution.py:37
  32.8 13.5 %convolution_convert_fusion = bf16[28800,128]{1,0:T(8,128)(2,1)S(1)} fusion(bf16[28800,512]{1,0:T(8,128)(2,1)} %multiply_convert_fusion.1, bf16[512,128]{1,0:T(8,128)(2,1)S(1)} %copy-done.4), kind=kOutput, calls=%fused_computation.34 | convolution fusion | flops 3778560000 | bytes 36995072 | tf_op jit(solution)/shard_map/dot_general | solution.py:66
  52.5 5.8 %collective-permute-start.1 = (bf16[4,640,128]{2,1,0:T(8,128)(2,1)}, bf16[4,640,128]{2,1,0:T(8,128)(2,1)S(1)}, u32[]{:S(2)}, u32[]{:S(2)}) collective-permute-start(bf16[4,640,128]{2,1,0:T(8,128)(2,1)} %bitcast.2), channel_id=1, source_target_pairs={{4,0},{8,4},{12,8},{16,12},{20,16},{24,20},{28,24},{32,28},{36,32}... | collective-permute-start | bytes 1966088 | tf_op jit(solution)/shard_map/ppermute | solution.py:19
  59.4 5.1 %all-to-all-start = ((bf16[4,640,128]{1,2,0:T(8,128)(2,1)}), bf16[4,640,128]{1,2,0:T(8,128)(2,1)S(1)}, u32[]{:S(2)}, u32[]{:S(2)}) async-start(bf16[4,640,128]{1,2,0:T(8,128)(2,1)} %stack.2), calls=%async_computation | async-start | bytes 1310720 | tf_op jit(solution)/shard_map/all_to_all | solution.py:76
  64.8 15.0 %all-to-all-done = bf16[4,640,128]{1,2,0:T(8,128)(2,1)S(1)} async-done(((bf16[4,640,128]{1,2,0:T(8,128)(2,1)}), bf16[4,640,128]{1,2,0:T(8,128)(2,1)S(1)}, u32[]{:S(2)}, u32[]{:S(2)}) %all-to-all-start) | async-done | bytes 655392 | tf_op jit(solution)/shard_map/all_to_all | solution.py:76
  80.2 4.3 %pad_maximum_fusion = bf16[53,640,128]{2,1,0:T(8,128)(2,1)S(1)} fusion(bf16[4,640,128]{2,1,0:T(8,128)(2,1)S(1)} %collective-permute-done.1, bf16[45,640,128]{2,1,0:T(8,128)(2,1)} %bitcast.50, bf16[4,640,128]{2,1,0:T(8,128)(2,1)S(1)} %collective-permute-done), kind=kLoop, calls=%fused_computation.35 | loop fusion | flops 8683520 | bytes 17367040 | tf_op jit(solution)/shard_map/concatenate | solution.py:20
  84.5 6.2 %bitcast_convert_fusion = f32[33920,128]{1,0:T(8,128)} fusion(bf16[53,640,128]{2,1,0:T(8,128)(2,1)S(1)} %pad_maximum_fusion), kind=kLoop, calls=%fused_computation.36 | loop fusion | flops 4341760 | bytes 26050560 | tf_op jit(solution)/shard_map/convert_element_type | solution.py:69
  90.7 231.8 %while.13 = (s32[]{:T(128)}, f32[640,128]{1,0:T(8,128)S(1)}, f32[640]{0:T(1024)S(1)}, s32[11,2048]{1,0:T(8,128)S(1)}, s32[11,2048]{1,0:T(8,128)S(1)}, /*index=5*...) while((s32[]{:T(128)}, f32[640,128]{1,0:T(8,128)S(1)}, ...), condition=%wide.region_2.3_spmd.clone, body=%wide.region_0.2_spmd.clone.sunk | while | flops 347021952 | bytes 7114884 | solution.py:118
  90.8 5.5 %gather_fusion = f32[2048,128]{1,0:T(8,128)S(1)} fusion(f32[640,128]{1,0:T(8,128)S(1)} %get-tuple-element.233, s32[2048]{0:T(1024)S(1)} %broadcast_clamp_fusion.4), kind=kCustom, calls=%fused_computation.1.clone.clone.1 | custom fusion | bytes 2105344 | tf_op jit(solution)/shard_map/while/body/eval_jaxpr/jit(_take)/gather | solution.py:90
  96.2 11.4 %gather_fusion.1 = f32[2048,128]{1,0:T(8,128)S(1)} fusion(f32[33920,128]{1,0:T(8,128)} %get-tuple-element.232, s32[2048]{0:T(1024)S(1)} %broadcast_clamp_fusion.5), kind=kCustom, calls=%fused_computation.clone.clone.1 | custom fusion | bytes 2105344 | tf_op jit(solution)/shard_map/while/body/eval_jaxpr/jit(_take)/gather | solution.py:90
  111.8 5.5 %gather_fusion = f32[2048,128]{1,0:T(8,128)S(1)} fusion(f32[640,128]{1,0:T(8,128)S(1)} %get-tuple-element.233, s32[2048]{0:T(1024)S(1)} %broadcast_clamp_fusion.4), kind=kCustom, calls=%fused_computation.1.clone.clone.1 | custom fusion | bytes 2105344 | tf_op jit(solution)/shard_map/while/body/eval_jaxpr/jit(_take)/gather | solution.py:90
  117.3 11.4 %gather_fusion.1 = f32[2048,128]{1,0:T(8,128)S(1)} fusion(f32[33920,128]{1,0:T(8,128)} %get-tuple-element.232, s32[2048]{0:T(1024)S(1)} %broadcast_clamp_fusion.5), kind=kCustom, calls=%fused_computation.clone.clone.1 | custom fusion | bytes 2105344 | tf_op jit(solution)/shard_map/while/body/eval_jaxpr/jit(_take)/gather | solution.py:90
  132.9 5.5 %gather_fusion = f32[2048,128]{1,0:T(8,128)S(1)} fusion(f32[640,128]{1,0:T(8,128)S(1)} %get-tuple-element.233, s32[2048]{0:T(1024)S(1)} %broadcast_clamp_fusion.4), kind=kCustom, calls=%fused_computation.1.clone.clone.1 | custom fusion | bytes 2105344 | tf_op jit(solution)/shard_map/while/body/eval_jaxpr/jit(_take)/gather | solution.py:90
  138.4 11.4 %gather_fusion.1 = f32[2048,128]{1,0:T(8,128)S(1)} fusion(f32[33920,128]{1,0:T(8,128)} %get-tuple-element.232, s32[2048]{0:T(1024)S(1)} %broadcast_clamp_fusion.5), kind=kCustom, calls=%fused_computation.clone.clone.1 | custom fusion | bytes 2105344 | tf_op jit(solution)/shard_map/while/body/eval_jaxpr/jit(_take)/gather | solution.py:90
  154.0 5.5 %gather_fusion = f32[2048,128]{1,0:T(8,128)S(1)} fusion(f32[640,128]{1,0:T(8,128)S(1)} %get-tuple-element.233, s32[2048]{0:T(1024)S(1)} %broadcast_clamp_fusion.4), kind=kCustom, calls=%fused_computation.1.clone.clone.1 | custom fusion | bytes 2105344 | tf_op jit(solution)/shard_map/while/body/eval_jaxpr/jit(_take)/gather | solution.py:90
  159.5 11.4 %gather_fusion.1 = f32[2048,128]{1,0:T(8,128)S(1)} fusion(f32[33920,128]{1,0:T(8,128)} %get-tuple-element.232, s32[2048]{0:T(1024)S(1)} %broadcast_clamp_fusion.5), kind=kCustom, calls=%fused_computation.clone.clone.1 | custom fusion | bytes 2105344 | tf_op jit(solution)/shard_map/while/body/eval_jaxpr/jit(_take)/gather | solution.py:90
  175.0 5.5 %gather_fusion = f32[2048,128]{1,0:T(8,128)S(1)} fusion(f32[640,128]{1,0:T(8,128)S(1)} %get-tuple-element.233, s32[2048]{0:T(1024)S(1)} %broadcast_clamp_fusion.4), kind=kCustom, calls=%fused_computation.1.clone.clone.1 | custom fusion | bytes 2105344 | tf_op jit(solution)/shard_map/while/body/eval_jaxpr/jit(_take)/gather | solution.py:90
  180.5 11.4 %gather_fusion.1 = f32[2048,128]{1,0:T(8,128)S(1)} fusion(f32[33920,128]{1,0:T(8,128)} %get-tuple-element.232, s32[2048]{0:T(1024)S(1)} %broadcast_clamp_fusion.5), kind=kCustom, calls=%fused_computation.clone.clone.1 | custom fusion | bytes 2105344 | tf_op jit(solution)/shard_map/while/body/eval_jaxpr/jit(_take)/gather | solution.py:90
  196.1 5.5 %gather_fusion = f32[2048,128]{1,0:T(8,128)S(1)} fusion(f32[640,128]{1,0:T(8,128)S(1)} %get-tuple-element.233, s32[2048]{0:T(1024)S(1)} %broadcast_clamp_fusion.4), kind=kCustom, calls=%fused_computation.1.clone.clone.1 | custom fusion | bytes 2105344 | tf_op jit(solution)/shard_map/while/body/eval_jaxpr/jit(_take)/gather | solution.py:90
  201.6 11.4 %gather_fusion.1 = f32[2048,128]{1,0:T(8,128)S(1)} fusion(f32[33920,128]{1,0:T(8,128)} %get-tuple-element.232, s32[2048]{0:T(1024)S(1)} %broadcast_clamp_fusion.5), kind=kCustom, calls=%fused_computation.clone.clone.1 | custom fusion | bytes 2105344 | tf_op jit(solution)/shard_map/while/body/eval_jaxpr/jit(_take)/gather | solution.py:90
  217.2 5.5 %gather_fusion = f32[2048,128]{1,0:T(8,128)S(1)} fusion(f32[640,128]{1,0:T(8,128)S(1)} %get-tuple-element.233, s32[2048]{0:T(1024)S(1)} %broadcast_clamp_fusion.4), kind=kCustom, calls=%fused_computation.1.clone.clone.1 | custom fusion | bytes 2105344 | tf_op jit(solution)/shard_map/while/body/eval_jaxpr/jit(_take)/gather | solution.py:90
  222.7 11.4 %gather_fusion.1 = f32[2048,128]{1,0:T(8,128)S(1)} fusion(f32[33920,128]{1,0:T(8,128)} %get-tuple-element.232, s32[2048]{0:T(1024)S(1)} %broadcast_clamp_fusion.5), kind=kCustom, calls=%fused_computation.clone.clone.1 | custom fusion | bytes 2105344 | tf_op jit(solution)/shard_map/while/body/eval_jaxpr/jit(_take)/gather | solution.py:90
  238.3 5.5 %gather_fusion = f32[2048,128]{1,0:T(8,128)S(1)} fusion(f32[640,128]{1,0:T(8,128)S(1)} %get-tuple-element.233, s32[2048]{0:T(1024)S(1)} %broadcast_clamp_fusion.4), kind=kCustom, calls=%fused_computation.1.clone.clone.1 | custom fusion | bytes 2105344 | tf_op jit(solution)/shard_map/while/body/eval_jaxpr/jit(_take)/gather | solution.py:90
  243.8 11.4 %gather_fusion.1 = f32[2048,128]{1,0:T(8,128)S(1)} fusion(f32[33920,128]{1,0:T(8,128)} %get-tuple-element.232, s32[2048]{0:T(1024)S(1)} %broadcast_clamp_fusion.5), kind=kCustom, calls=%fused_computation.clone.clone.1 | custom fusion | bytes 2105344 | tf_op jit(solution)/shard_map/while/body/eval_jaxpr/jit(_take)/gather | solution.py:90
  259.3 5.5 %gather_fusion = f32[2048,128]{1,0:T(8,128)S(1)} fusion(f32[640,128]{1,0:T(8,128)S(1)} %get-tuple-element.233, s32[2048]{0:T(1024)S(1)} %broadcast_clamp_fusion.4), kind=kCustom, calls=%fused_computation.1.clone.clone.1 | custom fusion | bytes 2105344 | tf_op jit(solution)/shard_map/while/body/eval_jaxpr/jit(_take)/gather | solution.py:90
  264.8 11.4 %gather_fusion.1 = f32[2048,128]{1,0:T(8,128)S(1)} fusion(f32[33920,128]{1,0:T(8,128)} %get-tuple-element.232, s32[2048]{0:T(1024)S(1)} %broadcast_clamp_fusion.5), kind=kCustom, calls=%fused_computation.clone.clone.1 | custom fusion | bytes 2105344 | tf_op jit(solution)/shard_map/while/body/eval_jaxpr/jit(_take)/gather | solution.py:90
  280.4 5.5 %gather_fusion = f32[2048,128]{1,0:T(8,128)S(1)} fusion(f32[640,128]{1,0:T(8,128)S(1)} %get-tuple-element.233, s32[2048]{0:T(1024)S(1)} %broadcast_clamp_fusion.4), kind=kCustom, calls=%fused_computation.1.clone.clone.1 | custom fusion | bytes 2105344 | tf_op jit(solution)/shard_map/while/body/eval_jaxpr/jit(_take)/gather | solution.py:90
  285.9 11.4 %gather_fusion.1 = f32[2048,128]{1,0:T(8,128)S(1)} fusion(f32[33920,128]{1,0:T(8,128)} %get-tuple-element.232, s32[2048]{0:T(1024)S(1)} %broadcast_clamp_fusion.5), kind=kCustom, calls=%fused_computation.clone.clone.1 | custom fusion | bytes 2105344 | tf_op jit(solution)/shard_map/while/body/eval_jaxpr/jit(_take)/gather | solution.py:90
  301.5 5.5 %gather_fusion = f32[2048,128]{1,0:T(8,128)S(1)} fusion(f32[640,128]{1,0:T(8,128)S(1)} %get-tuple-element.233, s32[2048]{0:T(1024)S(1)} %broadcast_clamp_fusion.4), kind=kCustom, calls=%fused_computation.1.clone.clone.1 | custom fusion | bytes 2105344 | tf_op jit(solution)/shard_map/while/body/eval_jaxpr/jit(_take)/gather | solution.py:90
  307.0 11.4 %gather_fusion.1 = f32[2048,128]{1,0:T(8,128)S(1)} fusion(f32[33920,128]{1,0:T(8,128)} %get-tuple-element.232, s32[2048]{0:T(1024)S(1)} %broadcast_clamp_fusion.5), kind=kCustom, calls=%fused_computation.clone.clone.1 | custom fusion | bytes 2105344 | tf_op jit(solution)/shard_map/while/body/eval_jaxpr/jit(_take)/gather | solution.py:90
  329.0 17.0 %all-to-all-done.1 = f32[4,640,128]{1,2,0:T(8,128)S(1)} async-done(((f32[4,640,128]{1,2,0:T(8,128)}), f32[4,640,128]{1,2,0:T(8,128)S(1)}, u32[]{:S(2)}, u32[]{:S(2)}) %all-to-all-start.1) | async-done | bytes 1310752 | tf_op jit(solution)/shard_map/all_to_all | solution.py:31
  346.3 7.5 %all-reduce = (f32[640,1]{0,1:T(1,128)S(1)}, f32[640,1]{0,1:T(1,128)S(1)}) all-reduce(f32[640,1]{0,1:T(1,128)S(1)} %broadcast_in_dim.39, f32[640,1]{0,1:T(1,128)S(1)} %broadcast_in_dim.40), channel_id=1, replica_groups=mesh['lon'=32,'ch'=4] {'ch'}, use_global_device_ids=true, to_apply=%region_5.6 | all-reduce | flops 1280 | bytes 10240 | tf_op jit(solution)/shard_map/psum | solution.py:124
  (137 shorter events, 62.0 us)
Async XLA Ops:
  0.0 1.0 copy-start
  0.0 32.8 %copy-start.4 = (bf16[512,128]{1,0:T(8,128)(2,1)S(1)}, bf16[512,128]{1,0:T(8,128)(2,1)}, u32[]{:S(2)}) copy-start(bf16[512,128]{1,0:T(8,128)(2,1)} %param.24) | copy-start | bytes 393220
  32.8 25.5 %copy-start.3 = (bf16[640,128]{1,0:T(8,128)(2,1)S(1)}, bf16[640,128]{1,0:T(8,128)(2,1)}, u32[]{:S(2)}) copy-start(bf16[640,128]{1,0:T(8,128)(2,1)} %param.20) | copy-start | bytes 491524
  32.8 31.7 %copy-start.7 = (s32[22528]{0:T(1024)S(1)}, s32[22528]{0:T(1024)}, u32[]{:S(2)}) copy-start(s32[22528]{0:T(1024)} %param.23) | copy-start | bytes 270340
  32.8 31.8 %copy-start.8 = (s32[22528]{0:T(1024)S(1)}, s32[22528]{0:T(1024)}, u32[]{:S(2)}) copy-start(s32[22528]{0:T(1024)} %param.22) | copy-start | bytes 270340
  32.8 47.0 %copy-start.5 = (bf16[512,128]{1,0:T(8,128)(2,1)S(1)}, bf16[512,128]{1,0:T(8,128)(2,1)}, u32[]{:S(2)}) copy-start(bf16[512,128]{1,0:T(8,128)(2,1)} %param.25) | copy-start | bytes 393220
  46.3 3.0 copy-start.2
  50.5 29.7 %collective-permute-start = (bf16[4,640,128]{2,1,0:T(8,128)(2,1)}, bf16[4,640,128]{2,1,0:T(8,128)(2,1)S(1)}, u32[]{:S(2)}, u32[]{:S(2)}) collective-permute-start(bf16[4,640,128]{2,1,0:T(8,128)(2,1)} %bitcast), channel_id=1, source_target_pairs={{0,4},{4,8},{8,12},{12,16},{16,20},{20,24},{24,28},{28,32},{32,36}... | collective-permute-start | bytes 1966088 | tf_op jit(solution)/shard_map/ppermute | solution.py:16
  52.5 27.7 %collective-permute-start.1 = (bf16[4,640,128]{2,1,0:T(8,128)(2,1)}, bf16[4,640,128]{2,1,0:T(8,128)(2,1)S(1)}, u32[]{:S(2)}, u32[]{:S(2)}) collective-permute-start(bf16[4,640,128]{2,1,0:T(8,128)(2,1)} %bitcast.2), channel_id=1, source_target_pairs={{4,0},{8,4},{12,8},{16,12},{20,16},{24,20},{28,24},{32,28},{36,32}... | collective-permute-start | bytes 1966088 | tf_op jit(solution)/shard_map/ppermute | solution.py:19
  59.4 20.4 %all-to-all-start = ((bf16[4,640,128]{1,2,0:T(8,128)(2,1)}), bf16[4,640,128]{1,2,0:T(8,128)(2,1)S(1)}, u32[]{:S(2)}, u32[]{:S(2)}) async-start(bf16[4,640,128]{1,2,0:T(8,128)(2,1)} %stack.2), calls=%async_computation | async-start | bytes 1310720 | tf_op jit(solution)/shard_map/all_to_all | solution.py:76
  84.5 6.2 %copy-start.11 = (bf16[4,128]{1,0:T(4,128)(2,1)S(1)}, bf16[4,128]{1,0:T(4,128)(2,1)}, u32[]{:S(2)}) copy-start(bf16[4,128]{1,0:T(4,128)(2,1)} %param.26) | copy-start | bytes 3076
  84.5 6.2 %copy-start.12 = (f32[128]{0:T(128)S(1)}, f32[128]{0:T(128)}, u32[]{:S(2)}) copy-start(f32[128]{0:T(128)} %param.27) | copy-start | bytes 1540
  90.7 231.8 %copy-start.6 = (bf16[128,512]{1,0:T(8,128)(2,1)S(1)}, bf16[128,512]{1,0:T(8,128)(2,1)}, u32[]{:S(2)}) copy-start(bf16[128,512]{1,0:T(8,128)(2,1)} %param.28) | copy-start | bytes 393220
  90.7 263.2 %copy-start.9 = (f32[128]{0:T(128)S(1)}, f32[128]{0:T(128)}, u32[]{:S(2)}) copy-start(f32[128]{0:T(128)} %param.31) | copy-start | bytes 1540
  90.7 263.2 %copy-start.10 = (f32[128]{0:T(128)S(1)}, f32[128]{0:T(128)}, u32[]{:S(2)}) copy-start(f32[128]{0:T(128)} %param.30) | copy-start | bytes 1540
  322.5 32.4 %copy-start.1 = (bf16[474,512]{1,0:T(8,128)(2,1)S(1)}, bf16[474,512]{1,0:T(8,128)(2,1)}, u32[]{:S(2)}) copy-start(bf16[474,512]{1,0:T(8,128)(2,1)} %param.18) | copy-start | bytes 1456132
  324.3 21.7 %all-to-all-start.1 = ((f32[4,640,128]{1,2,0:T(8,128)}), f32[4,640,128]{1,2,0:T(8,128)S(1)}, u32[]{:S(2)}, u32[]{:S(2)}) async-start(f32[4,640,128]{1,2,0:T(8,128)} %bitcast.9), calls=%async_computation.1 | async-start | bytes 2621440 | tf_op jit(solution)/shard_map/all_to_all | solution.py:31
